TPU v7x, 32 devices: a whole 2x2x4 slice. The times are simulated.
32 devices in a mesh: dp: 8 (over z, core), tensor: 4 (over y, x).
Axes of the slice: x: 2, y: 2, z: 4, core: 2. Of those that a mesh axis runs over, the one named last changes fastest.
Arguments:
- prompt_ids: int32 [4096], P(('dp', 'tensor')), may hold values from 0 to 128255
- prompt_lengths: int32 [8], replicated, may hold values from 1 to 512, as said below
- embed_table: bfloat16 [4096, 128256], P(('dp', 'tensor')), may hold values from -4 to 4
- norm_gain: float32 [4096], replicated, may hold values from 0.5 to 1.5
- w_query: bfloat16 [4096, 4096], P('dp', 'tensor'), may hold values from -3 to 3
- w_key: bfloat16 [4096, 1024], P('dp', 'tensor'), may hold values from -1 to 1
- w_value: bfloat16 [4096, 1024], P('dp', 'tensor'), may hold values from -0.09375 to 0.09375
- w_out: bfloat16 [4096, 4096], P('tensor', 'dp'), may hold values from -0.09375 to 0.09375
Outputs:
- hidden: bfloat16 [4096, 4096], P(('dp', 'tensor'))
- kv_cache: bfloat16 [32, 2, 512, 256], P(('dp', 'tensor'))
Inputs may be any that keep to these rules, and one draw needn't show every extreme that they name: `prompt_lengths`: each group's prompt has 1 to 512 live tokens, and some group's has 512.
All inputs are finite; a program needn't handle non-finite values.
Results may differ from a plain program's by a relative error of at most 0.0095.
Values may be sent and summed in bfloat16 or wider, within the bound.
A program may use at most 192 MiB of HBM per device.

v0:
```python
import jax
import jax.numpy as jnp
from jax import lax
from jax.sharding import PartitionSpec as P

HEADS = 32
KVH = 8
HD = 128
TPG = 4
norm_eps = 1e-05
rope_theta = 500000.0


def swapped(block, axis, apart):
    count = lax.axis_size(axis)
    route = []
    for low in range(count):
        high = low | 1 << apart
        if high != low and high < count:
            route += [(low, high), (high, low)]
    return lax.ppermute(block, axis, route)


def for_sending(shard):

    def short(part):
        return part.astype(jnp.bfloat16) if part.dtype == jnp.float32 else part

    return jax.tree.map(short, shard)


def rotate(heads_in, positions):
    half = heads_in.shape[-1] // 2
    freq = rope_theta ** (-2.0 * jnp.arange(half, dtype=jnp.float32) / heads_in.shape[-1])
    angle = positions.astype(jnp.float32)[:, None] * freq[None, :]
    cosine = jnp.cos(angle)[:, None, :]
    sine = jnp.sin(angle)[:, None, :]
    first = heads_in[..., :half]
    second = heads_in[..., half:]
    return jnp.concatenate(
        [first * cosine - second * sine, second * cosine + first * sine], axis=-1
    )


def attend(query_rot, key_rot, value_rows, length):
    row_count = query_rot.shape[0]
    block = min(512, row_count)
    positions = jnp.arange(row_count, dtype=jnp.int32)

    def one_block(offset):
        scores = jnp.einsum(
            "qhgd,khd->hgqk", query_rot, key_rot, preferred_element_type=jnp.float32
        ) / jnp.sqrt(jnp.float32(HD))
        query_pos = offset + jnp.arange(block, dtype=jnp.int32)
        allowed = (positions[None, :] <= query_pos[:, None]) & (positions[None, :] < length)
        scores = jnp.where(allowed, scores, -1e30)
        biggest = jnp.max(scores, axis=-1, keepdims=True)
        expd = jnp.exp(scores - biggest)
        weights = (expd / jnp.sum(expd, axis=-1, keepdims=True)).astype(jnp.bfloat16)
        result = jnp.einsum(
            "hgqk,khd->qhgd", weights, value_rows, preferred_element_type=jnp.float32
        )
        return result.astype(jnp.bfloat16)

    starts = jnp.arange(0, row_count, block, dtype=jnp.int32)
    outs = lax.map(one_block, starts)
    return outs.reshape(row_count, -1)


def ordered_pair(mine, theirs, bit_index):
    upper_half = lax.axis_index("tensor") >> bit_index & 1 == 1
    first_half = jnp.where(upper_half, theirs, mine)
    second_half = jnp.where(upper_half, mine, theirs)
    return jnp.concatenate([first_half, second_half], axis=0)


def collect_blocks(shard, swapper):
    stacked = shard[None]
    levels = lax.axis_size("tensor").bit_length() - 1
    for bit_index in range(TPG.bit_length() - 1, levels):
        stacked = ordered_pair(stacked, swapper(stacked, bit_index), bit_index)
    return stacked


def gather_in_group(own_part):
    joined = own_part
    for bit_index in range(TPG.bit_length() - 1):
        joined = ordered_pair(joined, swapped(joined, "tensor", bit_index), bit_index)
    return joined


def rms_normed(tokens_in, norm_gain):
    wide_in = tokens_in.astype(jnp.float32)
    scale = lax.rsqrt(jnp.mean(wide_in * wide_in, axis=1, keepdims=True) + norm_eps)
    return (wide_in * scale * norm_gain[None, :]).astype(jnp.bfloat16)


def lookup_rows(embed_table, token_ids):
    columns = embed_table.shape[0]
    vocab_size = embed_table.shape[1]
    packing = max(1, 128 // columns)
    token_major = embed_table.T.reshape(vocab_size // packing, packing * columns)
    fetched = jnp.take(token_major, token_ids // packing, axis=0).reshape(
        token_ids.shape[0], packing, columns
    )
    if packing == 1:
        return fetched.reshape(token_ids.shape[0], columns)
    slot_ids = jnp.arange(packing, dtype=jnp.int32)
    wanted = (token_ids % packing)[:, None] == slot_ids[None, :]
    chosen = jnp.where(wanted[:, :, None], fetched, jnp.zeros_like(fetched))
    return jnp.sum(chosen, axis=1, dtype=jnp.bfloat16)


def shards(prompt_ids, prompt_lengths, embed_table, norm_gain, w_query, w_key, w_value, w_out):
    quarter = prompt_ids.shape[0]
    row_count = quarter * TPG
    devices = lax.axis_size(("dp", "tensor"))
    columns = embed_table.shape[0]
    model_width = columns * devices
    group_index = (
        lax.axis_index("dp") * (lax.axis_size("tensor") // TPG) + lax.axis_index("tensor") // TPG
    )
    length = lax.dynamic_slice_in_dim(prompt_lengths, group_index, 1, 0)[0]
    all_ids = lax.all_gather(prompt_ids, ("dp", "tensor"), axis=0, tiled=True)
    picked = lookup_rows(embed_table, all_ids)
    outgoing = picked.reshape(devices, quarter, columns)
    arrived = lax.all_to_all(outgoing, ("dp", "tensor"), split_axis=0, concat_axis=2, tiled=True)
    own_rows = arrived.reshape(quarter, model_width)
    normed = gather_in_group(rms_normed(own_rows, norm_gain))
    query_width = w_query.shape[1]
    key_width = w_key.shape[1]
    packed = jnp.concatenate([w_query, w_key, w_value], axis=1)
    stacked = collect_blocks(
        packed,
        lambda values, bit_index: jax.tree.map(
            lambda part, own: part.astype(own.dtype),
            swapped(for_sending(values), "tensor", bit_index),
            values,
        ),
    )
    projected = jnp.einsum(
        "rd,kdc->rkc",
        normed,
        lax.all_gather(stacked, "dp", axis=1, tiled=True),
        preferred_element_type=jnp.float32,
    )
    blocks = projected.shape[1]
    local_heads = blocks * query_width // HD
    local_kv = blocks * key_width // HD
    positions = jnp.arange(row_count, dtype=jnp.int32)
    query = projected[:, :, :query_width].reshape(row_count, local_heads, HD)
    key_raw = projected[:, :, query_width : query_width + key_width].reshape(
        row_count, local_kv, HD
    )
    value_raw = projected[:, :, query_width + key_width :].reshape(row_count, local_kv, HD)
    query_rot = rotate(query, positions).astype(jnp.bfloat16)
    key_rot = rotate(key_raw, positions).astype(jnp.bfloat16)
    value_rows = value_raw.astype(jnp.bfloat16)
    cache = jnp.stack(
        [key_rot.reshape(row_count, local_kv * HD), value_rows.reshape(row_count, local_kv * HD)],
        axis=0,
    )[None]
    attended = attend(
        query_rot.reshape(row_count, local_kv, HEADS // KVH, HD), key_rot, value_rows, length
    )
    attended = attended.reshape(row_count, blocks, query_width)
    out_blocks = collect_blocks(
        w_out,
        lambda values, bit_index: jax.tree.map(
            lambda part, own: part.astype(own.dtype),
            swapped(for_sending(values), "tensor", bit_index),
            values,
        ),
    )
    partial_sum = jnp.einsum(
        "rkw,kwc->rc",
        attended,
        lax.all_gather(out_blocks, "dp", axis=2, tiled=True),
        preferred_element_type=jnp.float32,
    )
    levels_in = TPG.bit_length() - 1
    running = partial_sum
    for bit_index in reversed(range(levels_in)):
        half_rows = running.shape[0] // 2
        upper_half = lax.axis_index("tensor") >> bit_index & 1 == 1
        kept = jnp.where(upper_half, running[half_rows:], running[:half_rows]).astype(jnp.bfloat16)
        given = jnp.where(upper_half, running[:half_rows], running[half_rows:]).astype(jnp.bfloat16)
        arrived_sum = swapped(given, "tensor", bit_index)
        running = kept.astype(jnp.float32) + arrived_sum.astype(jnp.float32)
    hidden = (own_rows.astype(jnp.float32) + running).astype(jnp.bfloat16)
    return (hidden, cache)


def solution(mesh):
    in_specs = (
        P(("dp", "tensor")),
        P(),
        P(("dp", "tensor"), None),
        P(),
        P("dp", "tensor"),
        P("dp", "tensor"),
        P("dp", "tensor"),
        P("tensor", "dp"),
    )
    out_specs = (P(("dp", "tensor"), None), P(("dp", "tensor"), None, None, None))
    return jax.shard_map(shards, mesh=mesh, in_specs=in_specs, out_specs=out_specs, check_vma=False)
```

profile of v0, /device:TPU:28, one launch (start us, length us, event | category | flops | bytes accessed | tf_op | source)
XLA Modules:
  0.0 427.4 jit_solution(1103278415025191674)
XLA Ops:
  7.2 2.7 pad_maximum_fusion.1
  9.9 42.6 %copy.29 = bf16[128,128256]{0,1:T(8,128)(2,1)} copy(bf16[128,128256]{1,0:T(8,128)(2,1)} %param.10) | data formatting | bytes 65667072 | tf_op args[2]
  52.6 61.9 %all-gather.2 = s32[32,1,128]{2,1,0:T(1,128)S(1)} all-gather(s32[1,1,128]{2,1,0:T(1,128)S(1)} %bitcast.78), channel_id=1, replica_groups=mesh['dp'=8,'tensor'=4] {'dp','tensor'}, dimensions={0}, use_global_device_ids=true | all-gather | bytes 16896 | tf_op jit(solution)/shard_map/all_gather | solution.py:124
  114.5 43.0 %gather_fusion = bf16[4096,128]{1,0:T(8,128)(2,1)S(1)} fusion(bf16[128256,128]{1,0:T(8,128)(2,1)} %bitcast.67, s32[4096]{0:T(1024)S(1)} %fusion.24), kind=kCustom, calls=%fused_computation | custom fusion | bytes 2113536 | tf_op jit(solution)/shard_map/jit(_take)/gather | solution.py:103
  157.5 1.5 broadcast_select_fusion.4
  159.0 12.5 %all-to-all-start = ((bf16[32,128,128]{2,1,0:T(8,128)(2,1)}), bf16[32,128,128]{2,1,0:T(8,128)(2,1)S(1)}, u32[]{:S(2)}, u32[]{:S(2)}) async-start(bf16[32,128,128]{2,1,0:T(8,128)(2,1)} %broadcast_select_fusion.4), calls=%async_computation | async-start | bytes 2097152 | tf_op jit(solution)/shard_map/all_to_all | solution.py:127
  171.6 0.7 all-gather.8.cloned.1.call-update
  172.3 44.7 %all-to-all-done = bf16[32,128,128]{2,1,0:T(8,128)(2,1)S(1)} async-done(((bf16[32,128,128]{2,1,0:T(8,128)(2,1)}), bf16[32,128,128]{2,1,0:T(8,128)(2,1)S(1)}, u32[]{:S(2)}, u32[]{:S(2)}) %all-to-all-start) | async-done | bytes 1048608 | tf_op jit(solution)/shard_map/all_to_all | solution.py:127
  217.2 1.2 copy.30
  218.8 1.8 fusion.15
  220.6 1.2 collective-permute-start
  221.8 24.0 %collective-permute-done = bf16[128,4096]{1,0:T(8,128)(2,1)} collective-permute-done((bf16[128,4096]{1,0:T(8,128)(2,1)S(1)}, bf16[128,4096]{1,0:T(8,128)(2,1)}, u32[]{:S(2)}, u32[]{:S(2)}) %collective-permute-start) | collective-permute-done | bytes 1048608 | tf_op jit(solution)/shard_map/ppermute | solution.py:21
  245.8 3.0 broadcast_select_fusion.3
  248.9 1.7 pad_maximum_fusion
  250.8 0.6 dynamic_slice.6
  251.4 0.7 iota_compare_fusion.1
  252.0 0.8 fusion.22
  252.9 1.7 multiply_cosine_fusion
  254.6 42.9 %collective-permute-done.1 = bf16[256,4096]{1,0:T(8,128)(2,1)} collective-permute-done((bf16[256,4096]{1,0:T(8,128)(2,1)}, bf16[256,4096]{1,0:T(8,128)(2,1)}, u32[]{:S(2)}, u32[]{:S(2)}) %collective-permute-start.1) | collective-permute-done | bytes 2097184 | tf_op jit(solution)/shard_map/ppermute | solution.py:21
  297.5 5.1 %broadcast_select_fusion.1 = (bf16[256,4096]{1,0:T(8,128)(2,1)}, bf16[256,4096]{1,0:T(8,128)(2,1)}) fusion(bf16[256,4096]{1,0:T(8,128)(2,1)} %collective-permute-done.1, pred[]{:T(512)S(6)} %eq.9, bf16[128,4096]{1,0:T(8,128)(2,1)} %copy-done.1, bf16[128,4096]{1,0:T(8,128)(2,1)S(1)} %get-tuple-element.20), kind=kLoop, calls=%fused_computation.33 | loop fusion | flops 6291456 | bytes 8388609 | tf_op jit(solution)/shard_map/jit(_where)/select_n | solution.py:72
  302.6 10.6 %fusion.10 = f32[512,1,1536]{2,0,1:T(8,128)S(1)} fusion(bf16[4096,1536]{1,0:T(8,128)(2,1)} %all-gather.6.cloned.1.call-done, bf16[256,4096]{1,0:T(8,128)(2,1)} %get-tuple-element.17, bf16[256,4096]{1,0:T(8,128)(2,1)} %get-tuple-element.16), kind=kOutput, calls=%fused_computation.17 | convolution fusion | flops 6450839552 | bytes 19922944 | tf_op jit(solution)/shard_map/rd,kdc->rkc/dot_general | solution.py:141
  313.2 1.6 copy-done.4
  314.8 0.7 slice.83
  315.8 1.7 slice_bitcast_fusion
  317.6 0.5 copy.45
  318.1 0.5 copy-done.5
  318.5 0.9 subtract_convert_fusion
  319.4 1.2 copy.33
  320.6 1.1 copy.34
  321.8 0.8 copy.41
  322.6 0.6 fusion.29
  323.8 0.3 copy-done.3
  324.2 1.3 fusion.18
  325.5 5.6 %fusion.30 = (f32[2,4,512]{2,1,0:T(4,128)S(1)}, f32[2,4,512,512]{2,3,1,0:T(8,128)}) fusion(f32[2,512,512,4]{2,1,3,0:T(8,128)S(1)} %fusion.18, pred[512,512]{0,1:T(8,128)(4,1)S(1)} %copy-done.7), kind=kOutput, calls=%fused_computation.65 | output fusion | flops 12583423 | bytes 17055744 | tf_op jit(solution)/shard_map/while/body/eval_jaxpr/sub | solution.py:58
  331.2 4.1 fusion.17
  335.3 8.4 %fusion.31 = bf16[512,4096]{1,0:T(8,128)(2,1)S(1)} fusion(bf16[512,1024]{0,1:T(8,128)(2,1)S(1)} %bitcast.79, bf16[1024,4096]{1,0:T(8,128)(2,1)} %all-gather.8.cloned.1.call-done), kind=kOutput, calls=%fused_computation.67 | convolution fusion | flops 4294967296 | bytes 13631488 | tf_op jit(solution)/shard_map/rkw,kwc->rc/dot_general | solution.py:175
  344.0 0.4 collective-permute-start.2
  344.3 45.5 %collective-permute-done.2 = bf16[256,4096]{1,0:T(8,128)(2,1)S(1)} collective-permute-done((bf16[256,4096]{1,0:T(8,128)(2,1)S(1)}, bf16[256,4096]{1,0:T(8,128)(2,1)S(1)}, u32[]{:S(2)}, u32[]{:S(2)}) %collective-permute-start.2) | collective-permute-done | bytes 2097184 | tf_op jit(solution)/shard_map/ppermute | solution.py:21
  389.9 1.2 convert_add_fusion
  391.1 1.3 copy-done
  392.4 1.1 select_convert_fusion.2
  393.5 1.1 collective-permute-start.3
  394.6 1.0 copy.37
  395.6 1.1 convert_element_type.134
  396.7 1.1 slice_bitcast_fusion.1
  397.8 0.8 maximum_bitcast_fusion
  398.6 17.6 %collective-permute-done.3 = bf16[128,4096]{1,0:T(8,128)(2,1)S(1)} collective-permute-done((bf16[128,4096]{1,0:T(8,128)(2,1)}, bf16[128,4096]{1,0:T(8,128)(2,1)S(1)}, u32[]{:S(2)}, u32[]{:S(2)}) %collective-permute-start.3) | collective-permute-done | bytes 1048608 | tf_op jit(solution)/shard_map/ppermute | solution.py:21
  416.2 4.3 %fusion.16 = bf16[128,4096]{1,0:T(8,128)(2,1)} fusion(bf16[128,4096]{1,0:T(8,128)(2,1)S(1)} %collective-permute-done.3, f32[16,8,32,128]{3,2,1,0:T(8,128)S(1)} %bitcast.70, bf16[256,4096]{1,0:T(8,128)(2,1)} %copy-done, pred[]{:T(512)S(6)} %eq.8), kind=kLoop, calls=%fused_computation.25 | loop fusion | flops 3145728 | bytes 6291457 | tf_op jit(solution)/shard_map/convert_element_type | solution.py:190
  (38 shorter events, 2.1 us)
Async XLA Ops:
  7.2 295.4 %all-gather.6.cloned.1.call-start = ((), (), s32[]{:S(2)}) async-start(), calls=%async_computation.1 | async-start | bytes 14155776 | tf_op jit(solution)/shard_map/all_gather | solution.py:144
  9.9 42.7 %copy-start.10 = (s32[128]{0:T(128)S(1)}, s32[128]{0:T(128)}, u32[]{:S(2)}) copy-start(s32[128]{0:T(128)} %param.8) | copy-start | bytes 1540
  159.0 57.9 %all-to-all-start = ((bf16[32,128,128]{2,1,0:T(8,128)(2,1)}), bf16[32,128,128]{2,1,0:T(8,128)(2,1)S(1)}, u32[]{:S(2)}, u32[]{:S(2)}) async-start(bf16[32,128,128]{2,1,0:T(8,128)(2,1)} %broadcast_select_fusion.4), calls=%async_computation | async-start | bytes 2097152 | tf_op jit(solution)/shard_map/all_to_all | solution.py:127
  171.5 163.8 %all-gather.8.cloned.1.call-start = ((), (), s32[]{:S(2)}) async-start(), calls=%async_computation.2 | async-start | bytes 9437184 | tf_op jit(solution)/shard_map/all_gather | solution.py:178
  217.2 1.5 copy-start.9
  220.6 25.2 %collective-permute-start = (bf16[128,4096]{1,0:T(8,128)(2,1)S(1)}, bf16[128,4096]{1,0:T(8,128)(2,1)}, u32[]{:S(2)}, u32[]{:S(2)}) collective-permute-start(bf16[128,4096]{1,0:T(8,128)(2,1)S(1)} %fusion.15), channel_id=1, source_target_pairs={{0,1},{1,0},{2,3},{3,2},{4,5},{5,4},{6,7},{7,6},{8,9},{9,8},{10,11... | collective-permute-start | bytes 3145736 | tf_op jit(solution)/shard_map/ppermute | solution.py:21
  248.8 1.7 copy-start.1
  248.8 1.9 copy-start.11
  250.5 47.0 %collective-permute-start.1 = (bf16[256,4096]{1,0:T(8,128)(2,1)}, bf16[256,4096]{1,0:T(8,128)(2,1)}, u32[]{:S(2)}, u32[]{:S(2)}) collective-permute-start(bf16[256,4096]{1,0:T(8,128)(2,1)} %pad_maximum_fusion), channel_id=1, source_target_pairs={{0,2},{2,0},{1,3},{3,1},{4,6},{6,4},{5,7},{7,5},{8,10},{10,8},{9,1... | collective-permute-start | bytes 6291464 | tf_op jit(solution)/shard_map/ppermute | solution.py:21
  313.2 1.6 copy-start.4
  317.6 1.0 copy-start.5
  319.4 2.4 copy-start.6
  322.6 1.2 copy-start.2
  322.6 1.5 copy-start.3
  324.2 1.4 copy-start.7
  325.5 5.7 %copy-start.8 = (bf16[512,1,256]{0,2,1:T(8,128)(2,1)S(1)}, bf16[512,1,256]{0,2,1:T(8,128)(2,1)}, u32[]{:S(2)}) copy-start(bf16[512,1,256]{0,2,1:T(8,128)(2,1)} %copy.41) | copy-start | bytes 786436
  344.0 45.9 %collective-permute-start.2 = (bf16[256,4096]{1,0:T(8,128)(2,1)S(1)}, bf16[256,4096]{1,0:T(8,128)(2,1)S(1)}, u32[]{:S(2)}, u32[]{:S(2)}) collective-permute-start(bf16[256,4096]{1,0:T(8,128)(2,1)S(1)} %select_convert_fusion), channel_id=1, source_target_pairs={{0,2},{2,0},{1,3},{3,1},{4,6},{6,4},{5,7},{7,5},{8,10},{10,8},{9,1... | collective-permute-start | bytes 6291464 | tf_op jit(solution)/shard_map/ppermute | solution.py:21
  391.1 1.3 copy-start
  393.5 22.7 %collective-permute-start.3 = (bf16[128,4096]{1,0:T(8,128)(2,1)}, bf16[128,4096]{1,0:T(8,128)(2,1)S(1)}, u32[]{:S(2)}, u32[]{:S(2)}) collective-permute-start(bf16[128,4096]{1,0:T(8,128)(2,1)} %select_convert_fusion.2), channel_id=1, source_target_pairs={{0,1},{1,0},{2,3},{3,2},{4,5},{5,4},{6,7},{7,6},{8,9},{9,8},{10,11... | collective-permute-start | bytes 3145736 | tf_op jit(solution)/shard_map/ppermute | solution.py:21
Sparse Core Ops, SparseCore 0:
  10.0 114.7 all-gather.5
  173.9 90.8 all-gather.7
where the time goes:
time: 429 us; the launch traced here: 427 us
  waiting for transfers between devices  175 us (41%)
  local copies, waits for them, and re-layouts  102 us (24%)
  blocking collectives  61.9 us (14%)
  other arithmetic  34 us (8%)
  matrix products  24.5 us (6%)
  starting transfers between devices  15.5 us (4%)
  between operations  14.3 us (3%)
    ppermute x4, waiting for transfers between devices, swapped(): return lax.ppermute(block, axis, route)  130 us
    all_gather x1, blocking collectives, shards(): all_ids = lax.all_gather(prompt_ids, ('dp', 'tensor'), axis=0, tiled=True)  61.9 us
    unnamed x27, local copies, waits for them, and re-layouts  48.9 us
    all_to_all x1, waiting for transfers between devices, shards(): lax.all_to_all(outgoing, ('dp', 'tensor'), split_axis=0, concat_axis=2, t...  44.7 us
    gather x1, local copies, waits for them, and re-layouts, lookup_rows(): jnp.take(token_major, token_ids // packing, axis=0)  43 us
    all_to_all x1, starting transfers between devices, shards(): lax.all_to_all(outgoing, ('dp', 'tensor'), split_axis=0, concat_axis=2, t...  12.5 us
    dot_general x1, matrix products, shards(): jnp.einsum('rd,kdc->rkc', normed, lax.all_gather(stacked, 'dp', axis=1, t...  10.6 us
  transfers between devices with their start and end apart: 7, of which 5 were waited for; matrix products, arithmetic and copies ran while one was open for 32% of the time, Pallas kernels for 0%

commit v1 on v0

--- a/solution.py
+++ b/solution.py
@@ -124,7 +124,10 @@
     all_ids = lax.all_gather(prompt_ids, ("dp", "tensor"), axis=0, tiled=True)
     picked = lookup_rows(embed_table, all_ids)
     outgoing = picked.reshape(devices, quarter, columns)
-    arrived = lax.all_to_all(outgoing, ("dp", "tensor"), split_axis=0, concat_axis=2, tiled=True)
+    devices_2 = lax.axis_size(("dp", "tensor"))
+    shards_2 = jnp.stack(jnp.split(outgoing, devices_2, axis=0), axis=0)
+    shards_2 = lax.all_to_all(shards_2, ("dp", "tensor"), split_axis=0, concat_axis=0)
+    arrived = jnp.concatenate(shards_2, axis=2)
     own_rows = arrived.reshape(quarter, model_width)
     normed = gather_in_group(rms_normed(own_rows, norm_gain))
     query_width = w_query.shape[1]

time: 429 us -> 450 us (1.049)
  local copies, waits for them, and re-layouts: 102 us -> 121 us
    unnamed x27 -> x58, local copies, waits for them, and re-layouts: 48.9 us -> 68 us
  transfers between devices with their start and end apart: 7 -> 7, of which waited for: 5 -> 5; matrix products, arithmetic and copies ran while one was open for 32% -> 35% of each run, Pallas kernels for 0% -> 0%
where the time goes in v1:
time: 450 us; the launch traced here: 448 us
  waiting for transfers between devices  176 us (39%)
  local copies, waits for them, and re-layouts  121 us (27%)
  blocking collectives  61.9 us (14%)
  other arithmetic  34.7 us (8%)
  matrix products  24.5 us (5%)
  starting transfers between devices  15.4 us (3%)
  between operations  14.3 us (3%)
    ppermute x4, waiting for transfers between devices, swapped(): return lax.ppermute(block, axis, route)  130 us
    unnamed x58, local copies, waits for them, and re-layouts  68 us
    all_gather x1, blocking collectives, shards(): all_ids = lax.all_gather(prompt_ids, ('dp', 'tensor'), axis=0, tiled=True)  61.9 us
    all_to_all x1, waiting for transfers between devices, shards(): lax.all_to_all(shards_2, ('dp', 'tensor'), split_axis=0, concat_axis=0)  44.7 us
    gather x1, local copies, waits for them, and re-layouts, lookup_rows(): jnp.take(token_major, token_ids // packing, axis=0)  43 us
    all_to_all x1, starting transfers between devices, shards(): lax.all_to_all(shards_2, ('dp', 'tensor'), split_axis=0, concat_axis=0)  12.5 us
    dot_general x1, matrix products, shards(): jnp.einsum('rd,kdc->rkc', normed, lax.all_gather(stacked, 'dp', axis=1, t...  10.6 us
  transfers between devices with their start and end apart: 7, of which 5 were waited for; matrix products, arithmetic and copies ran while one was open for 35% of the time, Pallas kernels for 0%

profile of v1, /device:TPU:28, one launch (start us, length us, event | category | flops | bytes accessed | tf_op | source)
XLA Modules:
  0.0 447.8 jit_solution(745390748643489515)
XLA Ops:
  7.2 2.7 pad_maximum_fusion.1
  9.9 42.6 %copy.19 = bf16[128,128256]{0,1:T(8,128)(2,1)} copy(bf16[128,128256]{1,0:T(8,128)(2,1)} %param.10) | data formatting | bytes 65667072 | tf_op args[2]
  52.6 61.9 %all-gather.2 = s32[32,1,128]{2,1,0:T(1,128)S(1)} all-gather(s32[1,1,128]{2,1,0:T(1,128)S(1)} %bitcast.200), channel_id=1, replica_groups=mesh['dp'=8,'tensor'=4] {'dp','tensor'}, dimensions={0}, use_global_device_ids=true | all-gather | bytes 16896 | tf_op jit(solution)/shard_map/all_gather | solution.py:124
  114.5 43.0 %gather_fusion = bf16[4096,128]{1,0:T(8,128)(2,1)S(1)} fusion(bf16[128256,128]{1,0:T(8,128)(2,1)} %bitcast.190, s32[4096]{0:T(1024)S(1)} %fusion.24), kind=kCustom, calls=%fused_computation | custom fusion | bytes 2113536 | tf_op jit(solution)/shard_map/jit(_take)/gather | solution.py:103
  157.5 2.1 broadcast_select_fusion.2
  159.7 0.6 constant_dynamic-update-slice_fusion.31
  160.3 0.6 constant_dynamic-update-slice_fusion.30
  162.2 0.6 constant_dynamic-update-slice_fusion.27
  166.5 0.6 constant_dynamic-update-slice_fusion.20
  173.9 0.6 constant_dynamic-update-slice_fusion.8
  178.2 0.6 constant_dynamic-update-slice_fusion.1
  179.5 12.5 %all-to-all-start = ((bf16[32,1,128,128]{3,2,1,0:T(8,128)(2,1)}), bf16[32,1,128,128]{3,2,1,0:T(8,128)(2,1)S(1)}, u32[]{:S(2)}, u32[]{:S(2)}) async-start(bf16[32,1,128,128]{3,2,1,0:T(8,128)(2,1)} %constant_dynamic-update-slice_fusion), calls=%async_computation | async-start | bytes 2097152 | tf_op jit(solution)/shard_map/all_to_all | solution.py:129
  192.0 0.7 all-gather.8.cloned.1.call-update
  192.7 44.7 %all-to-all-done = bf16[32,1,128,128]{3,2,1,0:T(8,128)(2,1)S(1)} async-done(((bf16[32,1,128,128]{3,2,1,0:T(8,128)(2,1)}), bf16[32,1,128,128]{3,2,1,0:T(8,128)(2,1)S(1)}, u32[]{:S(2)}, u32[]{:S(2)}) %all-to-all-start) | async-done | bytes 1048608 | tf_op jit(solution)/shard_map/all_to_all | solution.py:129
  237.6 1.2 copy.20
  239.2 1.8 fusion.15
  241.0 1.2 collective-permute-start
  242.3 24.0 %collective-permute-done = bf16[128,4096]{1,0:T(8,128)(2,1)} collective-permute-done((bf16[128,4096]{1,0:T(8,128)(2,1)S(1)}, bf16[128,4096]{1,0:T(8,128)(2,1)}, u32[]{:S(2)}, u32[]{:S(2)}) %collective-permute-start) | collective-permute-done | bytes 1048608 | tf_op jit(solution)/shard_map/ppermute | solution.py:21
  266.3 3.0 broadcast_select_fusion.4
  269.3 1.7 pad_maximum_fusion
  271.8 0.7 iota_compare_fusion.1
  272.4 0.8 fusion.22
  273.3 1.7 multiply_cosine_fusion
  275.0 42.9 %collective-permute-done.1 = bf16[256,4096]{1,0:T(8,128)(2,1)} collective-permute-done((bf16[256,4096]{1,0:T(8,128)(2,1)}, bf16[256,4096]{1,0:T(8,128)(2,1)}, u32[]{:S(2)}, u32[]{:S(2)}) %collective-permute-start.1) | collective-permute-done | bytes 2097184 | tf_op jit(solution)/shard_map/ppermute | solution.py:21
  317.9 5.1 %broadcast_select_fusion.1 = (bf16[256,4096]{1,0:T(8,128)(2,1)}, bf16[256,4096]{1,0:T(8,128)(2,1)}) fusion(bf16[256,4096]{1,0:T(8,128)(2,1)} %collective-permute-done.1, pred[]{:T(512)S(6)} %eq.9, bf16[128,4096]{1,0:T(8,128)(2,1)} %copy-done.1, bf16[128,4096]{1,0:T(8,128)(2,1)S(1)} %get-tuple-element.20), kind=kLoop, calls=%fused_computation.33 | loop fusion | flops 6291456 | bytes 8388609 | tf_op jit(solution)/shard_map/jit(_where)/select_n | solution.py:72
  323.0 10.6 %fusion.10 = f32[512,1,1536]{2,0,1:T(8,128)S(1)} fusion(bf16[4096,1536]{1,0:T(8,128)(2,1)} %all-gather.6.cloned.1.call-done, bf16[256,4096]{1,0:T(8,128)(2,1)} %get-tuple-element.17, bf16[256,4096]{1,0:T(8,128)(2,1)} %get-tuple-element.16), kind=kOutput, calls=%fused_computation.17 | convolution fusion | flops 6450839552 | bytes 19922944 | tf_op jit(solution)/shard_map/rd,kdc->rkc/dot_general | solution.py:144
  333.7 1.6 copy-done.4
  335.2 0.7 slice.115
  336.3 1.7 slice_bitcast_fusion
  338.9 0.9 subtract_convert_fusion
  339.8 1.2 copy.23
  341.0 1.1 copy.24
  342.2 0.8 copy.31
  344.6 1.3 fusion.18
  345.9 5.6 %fusion.30 = (f32[2,4,512]{2,1,0:T(4,128)S(1)}, f32[2,4,512,512]{2,3,1,0:T(8,128)}) fusion(f32[2,512,512,4]{2,1,3,0:T(8,128)S(1)} %fusion.18, pred[512,512]{0,1:T(8,128)(4,1)S(1)} %copy-done.7), kind=kOutput, calls=%fused_computation.129 | output fusion | flops 12583423 | bytes 17055744 | tf_op jit(solution)/shard_map/while/body/eval_jaxpr/sub | solution.py:58
  351.6 4.1 fusion.17
  355.7 8.4 %fusion.31 = bf16[512,4096]{1,0:T(8,128)(2,1)S(1)} fusion(bf16[512,1024]{0,1:T(8,128)(2,1)S(1)} %bitcast.201, bf16[1024,4096]{1,0:T(8,128)(2,1)} %all-gather.8.cloned.1.call-done), kind=kOutput, calls=%fused_computation.131 | convolution fusion | flops 4294967296 | bytes 13631488 | tf_op jit(solution)/shard_map/rkw,kwc->rc/dot_general | solution.py:178
  364.7 45.6 %collective-permute-done.2 = bf16[256,4096]{1,0:T(8,128)(2,1)S(1)} collective-permute-done((bf16[256,4096]{1,0:T(8,128)(2,1)S(1)}, bf16[256,4096]{1,0:T(8,128)(2,1)S(1)}, u32[]{:S(2)}, u32[]{:S(2)}) %collective-permute-start.2) | collective-permute-done | bytes 2097184 | tf_op jit(solution)/shard_map/ppermute | solution.py:21
  410.3 1.2 convert_add_fusion
  411.5 1.3 copy-done
  412.9 1.1 select_convert_fusion.2
  413.9 1.0 collective-permute-start.3
  415.0 1.0 copy.27
  415.9 1.1 convert_element_type.129
  417.1 1.1 slice_bitcast_fusion.33
  418.1 0.8 maximum_bitcast_fusion
  419.0 17.7 %collective-permute-done.3 = bf16[128,4096]{1,0:T(8,128)(2,1)S(1)} collective-permute-done((bf16[128,4096]{1,0:T(8,128)(2,1)}, bf16[128,4096]{1,0:T(8,128)(2,1)S(1)}, u32[]{:S(2)}, u32[]{:S(2)}) %collective-permute-start.3) | collective-permute-done | bytes 1048608 | tf_op jit(solution)/shard_map/ppermute | solution.py:21
  436.7 4.3 fusion.16
  (70 shorter events, 20.9 us)
Async XLA Ops:
  7.2 315.8 %all-gather.6.cloned.1.call-start = ((), (), s32[]{:S(2)}) async-start(), calls=%async_computation.1 | async-start | bytes 14155776 | tf_op jit(solution)/shard_map/all_gather | solution.py:147
  9.9 42.7 %copy-start.10 = (s32[128]{0:T(128)S(1)}, s32[128]{0:T(128)}, u32[]{:S(2)}) copy-start(s32[128]{0:T(128)} %param.8) | copy-start | bytes 1540
  179.5 57.9 %all-to-all-start = ((bf16[32,1,128,128]{3,2,1,0:T(8,128)(2,1)}), bf16[32,1,128,128]{3,2,1,0:T(8,128)(2,1)S(1)}, u32[]{:S(2)}, u32[]{:S(2)}) async-start(bf16[32,1,128,128]{3,2,1,0:T(8,128)(2,1)} %constant_dynamic-update-slice_fusion), calls=%async_computation | async-start | bytes 2097152 | tf_op jit(solution)/shard_map/all_to_all | solution.py:129
  191.9 163.8 %all-gather.8.cloned.1.call-start = ((), (), s32[]{:S(2)}) async-start(), calls=%async_computation.2 | async-start | bytes 9437184 | tf_op jit(solution)/shard_map/all_gather | solution.py:181
  237.6 1.5 copy-start.9
  241.0 25.2 %collective-permute-start = (bf16[128,4096]{1,0:T(8,128)(2,1)S(1)}, bf16[128,4096]{1,0:T(8,128)(2,1)}, u32[]{:S(2)}, u32[]{:S(2)}) collective-permute-start(bf16[128,4096]{1,0:T(8,128)(2,1)S(1)} %fusion.15), channel_id=1, source_target_pairs={{0,1},{1,0},{2,3},{3,2},{4,5},{5,4},{6,7},{7,6},{8,9},{9,8},{10,11... | collective-permute-start | bytes 3145736 | tf_op jit(solution)/shard_map/ppermute | solution.py:21
  269.2 1.7 copy-start.1
  269.2 1.9 copy-start.11
  270.9 47.0 %collective-permute-start.1 = (bf16[256,4096]{1,0:T(8,128)(2,1)}, bf16[256,4096]{1,0:T(8,128)(2,1)}, u32[]{:S(2)}, u32[]{:S(2)}) collective-permute-start(bf16[256,4096]{1,0:T(8,128)(2,1)} %pad_maximum_fusion), channel_id=1, source_target_pairs={{0,2},{2,0},{1,3},{3,1},{4,6},{6,4},{5,7},{7,5},{8,10},{10,8},{9,1... | collective-permute-start | bytes 6291464 | tf_op jit(solution)/shard_map/ppermute | solution.py:21
  333.6 1.6 copy-start.4
  338.0 1.0 copy-start.5
  339.8 2.4 copy-start.6
  343.0 1.2 copy-start.2
  343.0 1.5 copy-start.3
  344.6 1.4 copy-start.7
  345.9 5.7 %copy-start.8 = (bf16[512,1,256]{0,2,1:T(8,128)(2,1)S(1)}, bf16[512,1,256]{0,2,1:T(8,128)(2,1)}, u32[]{:S(2)}) copy-start(bf16[512,1,256]{0,2,1:T(8,128)(2,1)} %copy.31) | copy-start | bytes 786436
  364.4 45.9 %collective-permute-start.2 = (bf16[256,4096]{1,0:T(8,128)(2,1)S(1)}, bf16[256,4096]{1,0:T(8,128)(2,1)S(1)}, u32[]{:S(2)}, u32[]{:S(2)}) collective-permute-start(bf16[256,4096]{1,0:T(8,128)(2,1)S(1)} %select_convert_fusion), channel_id=1, source_target_pairs={{0,2},{2,0},{1,3},{3,1},{4,6},{6,4},{5,7},{7,5},{8,10},{10,8},{9,1... | collective-permute-start | bytes 6291464 | tf_op jit(solution)/shard_map/ppermute | solution.py:21
  411.5 1.3 copy-start
  413.9 22.7 %collective-permute-start.3 = (bf16[128,4096]{1,0:T(8,128)(2,1)}, bf16[128,4096]{1,0:T(8,128)(2,1)S(1)}, u32[]{:S(2)}, u32[]{:S(2)}) collective-permute-start(bf16[128,4096]{1,0:T(8,128)(2,1)} %select_convert_fusion.2), channel_id=1, source_target_pairs={{0,1},{1,0},{2,3},{3,2},{4,5},{5,4},{6,7},{7,6},{8,9},{9,8},{10,11... | collective-permute-start | bytes 3145736 | tf_op jit(solution)/shard_map/ppermute | solution.py:21
Sparse Core Ops, SparseCore 0:
  10.0 114.7 all-gather.5
  194.4 90.8 all-gather.7
